TPU v7x, 32 devices: a whole 2x2x4 slice. The times are simulated.
32 devices in a mesh: bl: 8 (over y, x, core), bp: 4 (over z).
Axes of the slice: x: 2, y: 2, z: 4, core: 2. Of those that a mesh axis runs over, the one named last changes fastest.
Arguments:
- inverse_cov: float32 [8, 1024, 1024], P('bl', 'bp'), may hold values from -1 to 12, as said below
- channel_keep_mask: int32 [8, 1024], P('bl'), may hold values 0 or 1
- partner_ids: int32 [8, 2], P('bl'), may hold values from -1 to 7, as said below
- band_starts: int32 [2, 64], replicated, may hold values from 0 to 384
Outputs:
- fisher: float32 [2, 64, 64], P(None, 'bp', 'bl')
Inputs may be any that keep to these rules, and one draw needn't show every extreme that they name: partner_ids[i, k] is -1 for an empty slot, else the index of a baseline whose group, its index // 1, lies 1 to 4 groups after the group of baseline i, counted cyclically over the 8 groups; in every draw some baseline has all 2 slots filled. Each inverse_cov[i] is symmetric.
All inputs are finite; a program needn't handle non-finite values. No bound on the sum of `channel_keep_mask` on one device may be relied on, other than what follows from the above.
Results may differ from a plain program's by a relative error of at most 0.0003.
Values sent between devices are 32-bit elements; how exact they have to be, the bound alone decides.
A program may use at most 128 MiB of HBM per device.

v0:
```python
from functools import partial

import jax
import jax.numpy as jnp
from jax import lax
from jax.experimental import pallas as pl
from jax.experimental.pallas import tpu as pltpu
from jax.sharding import PartitionSpec as P

WINDOW_LENGTH = 128
KINDS = 4
CHUNKS = 8
PARTS = ((0, 4), (4, 8))
MESH = pl.DeviceIdType.MESH
NT = (((1,), (1,)), ((), ()))
NN = (((1,), (0,)), ((), ()))


def split(value):
    high = value.astype(jnp.bfloat16)
    return high, (value - high.astype(jnp.float32)).astype(jnp.bfloat16)


def dot(left, right, dims):
    return lax.dot_general(left, right, dims, preferred_element_type=jnp.float32)


def dot3(left, right, dims):
    return dot(left[0], right[0], dims) + (dot(left[0], right[1], dims) + dot(left[1], right[0], dims))


def exact(left, right, dims):
    return lax.dot_general(
        left, right, dims, precision=lax.Precision.HIGHEST, preferred_element_type=jnp.float32
    )


def column_of(row, length, offset):
    shape = (length, row.shape[1])
    spot = lax.broadcasted_iota(jnp.int32, shape, 0) + offset == lax.broadcasted_iota(jnp.int32, shape, 1)
    return jnp.sum(jnp.where(spot, row, 0.0), axis=1, keepdims=True)


def kernel(
    sizes, cov_ref, mask_ref, partner_ref, starts_ref, out_ref,
    raw, masks, partner_row, starts, panel, turn, near, far, sib_own, sib_near, sib_far, toep, toep_low, grown, felt,
    windows, ramp, edge, edge_own, crossed, tiles, landed,
    load_sem, sib_sem, turn_sem, far_sem, near_sem, sfar_sem, snear_sem, fin_send, fin_recv, ready,
):
    groups, owners, rows, width, bands = sizes
    window = WINDOW_LENGTH
    me, level = lax.axis_index("bl"), lax.axis_index("bp")
    per_half = width // rows
    half, first = level // per_half, pl.multiple_of(level % per_half * rows, rows)
    pair, core = me // 2, me % 2
    pairs = groups // 2
    sibling = pair * 2 + 1 - core
    beside = (pair + 1 - 2 * (pair % 2)) * 2 + core
    behind = (pair + pairs - 2) % pairs * 2 + core
    level_other = level // per_half * per_half + (per_half - 1 - level % per_half)
    tile_rows = bands // groups
    band_share = bands // owners
    step = rows // CHUNKS

    half_columns = pl.ds(pl.multiple_of(half * width, width), width)
    loads = [
        pltpu.make_async_copy(source, target, load_sem.at[index])
        for index, (source, target) in enumerate([
            (cov_ref.at[0, :, half_columns], raw),
            (mask_ref, masks),
            (starts_ref, starts),
            (partner_ref, partner_row),
        ])
    ]
    for load in loads:
        load.start()
    barrier = pltpu.get_barrier_semaphore()
    for d in range(1, groups):
        pl.semaphore_signal(barrier, inc=1, device_id=((me + d) % groups, level), device_id_type=MESH)
    for d in range(1, owners):
        pl.semaphore_signal(barrier, inc=1, device_id=(me, (level + d) % owners), device_id_type=MESH)
    for load in loads:
        load.wait()

    marks = masks[:, half_columns].astype(jnp.float32)
    row_marks = column_of(marks, rows, first)
    panel[...] = raw[...] * row_marks * marks
    pl.semaphore_wait(barrier, groups + owners - 2)

    def remote(source, target, sems, index, device):
        return pltpu.make_async_remote_copy(
            src_ref=source, dst_ref=target, send_sem=sems.at[0, index], recv_sem=sems.at[1, index],
            device_id=device, device_id_type=MESH,
        )

    def own_at(q):
        return panel.at[pl.ds(q * step, step)]

    def part(ref, q):
        return ref.at[pl.ds(q * step, step)]

    to_far = [remote(own_at(q), part(far, q), far_sem, q, (behind, level)) for q in range(CHUNKS)]
    near_direct = [remote(own_at(q), part(near, q), near_sem, q, (beside, level)) for q in range(CHUNKS)]
    near_relay = [remote(part(far, q), part(near, q), near_sem, q, (beside, level)) for q in range(CHUNKS)]
    far_on = [remote(part(far, q), part(sib_far, q), sfar_sem, q, (sibling, level)) for q in range(CHUNKS)]
    near_on = [remote(part(near, q), part(sib_near, q), snear_sem, q, (sibling, level)) for q in range(CHUNKS)]
    mine = pl.ds(first, rows)
    theirs = pl.ds(pl.multiple_of(width - rows - first, rows), rows)
    to_sibling = remote(panel, sib_own, sib_sem, 0, (sibling, level))
    to_turn = remote(panel.at[:, mine], turn, turn_sem, 0, (me, level_other))

    odd = pair % 2 == 1
    for q in range(CHUNKS):
        to_far[q].start()

        @pl.when(odd)
        def _():
            near_direct[q].start()

    to_turn.start()
    to_sibling.start()
    for d in range(1, groups):
        pl.semaphore_signal(ready, inc=1, device_id=((me + d) % groups, level), device_id_type=MESH)

    def relay(q):
        to_far[q].wait_recv()

        @pl.when(jnp.logical_not(odd))
        def _():
            near_relay[q].start()

        far_on[q].start()

    def forward(q):
        near_direct[q].wait_recv()
        near_on[q].start()

    far_apart = jnp.abs(
        lax.broadcasted_iota(jnp.int32, (rows, rows), 0) - lax.broadcasted_iota(jnp.int32, (rows, rows), 1)
    ).astype(jnp.float32)
    for kind in range(KINDS):
        toep[kind], toep_low[kind] = split(jnp.exp(far_apart * (-1.0 / (1 + kind))))
    toeplitz = [(toep[kind], toep_low[kind]) for kind in range(KINDS)]

    start = column_of(starts[pl.ds(half, 1), :].astype(jnp.float32), bands, 0)
    band_ids = lax.broadcasted_iota(jnp.int32, (bands, 1), 0)
    inverse_length = 1.0 / (1.0 + (band_ids % KINDS).astype(jnp.float32))
    channel = lax.broadcasted_iota(jnp.int32, (bands, width), 1).astype(jnp.float32)
    ahead = channel - start
    past = ahead - (window - 1)
    within = jnp.logical_and(ahead >= 0.0, past <= 0.0)
    for kind in range(KINDS):
        windows[kind] = jnp.where(jnp.logical_and(within, band_ids % KINDS == kind), 1.0, 0.0).astype(jnp.bfloat16)
    windows[KINDS] = jnp.where(within, 1.0, 0.0).astype(jnp.bfloat16)
    rise, fall = jnp.exp(-jnp.abs(ahead) * inverse_length), jnp.exp(-jnp.abs(past) * inverse_length)
    ramp[0:bands, :] = jnp.where(within, rise, 0.0)
    ramp[bands:, :] = jnp.where(within, fall, 0.0)
    edge[0:bands, :] = jnp.where(ahead < 0.0, rise, 0.0)
    edge[bands:2 * bands, :] = jnp.where(past > 0.0, fall, 0.0)
    carry_ids = lax.broadcasted_iota(jnp.int32, (2 * KINDS, 1), 0)
    carry_length = 1.0 / (1.0 + (carry_ids % KINDS).astype(jnp.float32))
    carry_channel = lax.broadcasted_iota(jnp.int32, (2 * KINDS, width), 1).astype(jnp.float32) - rows
    upper = carry_ids < KINDS
    carry_gap = jnp.where(upper, carry_channel, -1.0 - carry_channel)
    edge[2 * bands:, :] = jnp.where(carry_gap >= 0.0, jnp.exp(-jnp.abs(carry_gap) * carry_length), 0.0)

    own_split = split(panel[...])
    relay(0)
    for kind in range(KINDS):
        grown[kind] = dot3(toeplitz[kind], own_split, NN)
    relay(1)
    edges = split(edge[...])
    edges_mine, edges_theirs = split(edge[:, mine]), split(edge[:, theirs])
    square, aside = split(panel[:, mine]), split(panel[:, theirs])
    edge_own[:, mine] = dot3(edges_mine, square, NN) + dot3(edges_theirs, aside, NT)
    relay(2)
    edge_own[:, theirs] = dot3(edges_mine, aside, NN)
    relay(3)
    to_turn.wait_recv()
    edge_own[:, theirs] = edge_own[:, theirs] + dot3(edges_theirs, split(turn[...]), NN)
    ramps = split(ramp[...])
    place = lax.broadcasted_iota(jnp.int32, (rows, 1), 0)
    reach_in = jnp.where(first == 0, rows - place, place + 1).astype(jnp.float32)
    for kind in range(KINDS):
        carry = jnp.where(
            first == 0,
            edge_own[2 * bands + kind:2 * bands + kind + 1, :],
            edge_own[2 * bands + KINDS + kind:2 * bands + KINDS + kind + 1, :],
        )
        grown[kind] = grown[kind] + jnp.exp(reach_in * (-1.0 / (1 + kind))) * carry
        felt[kind] = dot3(split(grown[kind]), ramps, NT)
        if kind == 1:
            relay(4)
    own_edges = edge_own[0:2 * bands, :]
    across = dot3(split(own_edges), ramps, NT)
    relay(5)
    for q in range(PARTS[0][1]):
        forward(q)
    relay(6)
    to_sibling.wait_recv()

    def weight(baseline):
        return jnp.sum(jnp.where(partner_row[...] == baseline, 1.0, 0.0), axis=1, keepdims=True)

    pair_near, pair_far = (pair + 1) % pairs * 2, (pair + 2) % pairs * 2
    weights = [
        (sib_own, weight(sibling)), (near, weight(pair_near + core)), (far, weight(pair_far + core)),
        (sib_near, weight(pair_near + 1 - core)), (sib_far, weight(pair_far + 1 - core)),
    ]
    lane = lax.broadcasted_iota(jnp.int32, (1, rows), 1)

    def join(part_index, total, chores):
        begin, end = PARTS[part_index]
        span, low_row = (end - begin) * step, begin * step
        for q in range(begin, end):
            far_on[q].wait_recv()
            near_on[q].wait_recv()
        here = slice(low_row, low_row + span)
        summed = sum(ref[here, :] * factor for ref, factor in weights)
        partners = split(summed)
        ramp_here = split(ramp[:, mine][:, here])
        leak = dot3(partners, edges, NT)
        leak_bands = leak[:, 0:2 * bands]
        inner = dot3(ramp_here, split(leak_bands), NN)
        sums = jnp.zeros((KINDS * span, bands), jnp.float32)
        for kind in range(KINDS):
            if kind < len(chores):
                chores[kind]()
            left = dot3((partners[0][:, 0:rows], partners[1][:, 0:rows]), toeplitz[kind], NN)
            left = left + leak[:, 2 * bands + kind:2 * bands + kind + 1] * jnp.exp(
                (rows - lane).astype(jnp.float32) * (-1.0 / (1 + kind)))
            right = dot3((partners[0][:, rows:], partners[1][:, rows:]), toeplitz[kind], NN)
            right = right + leak[:, 2 * bands + KINDS + kind:2 * bands + KINDS + kind + 1] * jnp.exp(
                (lane + 1).astype(jnp.float32) * (-1.0 / (1 + kind)))
            turned = jnp.concatenate([left, right], axis=1)
            pieces = [split(grown[m, here, :] * turned) for m in range(KINDS)]
            stacked = jnp.concatenate([p[0] for p in pieces] + [p[1] for p in pieces], axis=0)
            boxed = dot(stacked, windows[kind], NT)
            sums = sums + (boxed[0:KINDS * span] + boxed[KINDS * span:])
            found = dot3(ramp_here, split(turned), NN)
            crossed[kind] = found if part_index == 0 else crossed[kind] + found
        inside_here = windows[KINDS, :, mine][:, here]
        for m in range(KINDS):
            reach = leak_bands * felt[m, here, :]
            high, low = split(sums[m * span:(m + 1) * span] - reach[:, 0:bands] - reach[:, bands:])
            total = total + jnp.where(
                band_ids % KINDS == m, dot(inside_here, high, NN) + dot(inside_here, low, NN), 0.0)
        return inner, total

    done, relayed = PARTS[0][1], 7
    inner, total = 0.0, jnp.zeros((bands, bands), jnp.float32)
    for part_index in range(len(PARTS)):
        chores = []
        if part_index + 1 < len(PARTS):
            chores = [partial(relay, q) for q in range(relayed, CHUNKS)]
            chores += [partial(forward, q) for q in range(done, PARTS[part_index + 1][1])]
            relayed, done = CHUNKS, PARTS[part_index + 1][1]
        found, total = join(part_index, total, chores[:KINDS])
        inner = inner + found
        for chore in chores[KINDS:]:
            chore()
    cross = inner * across
    total = total + cross[0:bands, 0:bands] + cross[0:bands, bands:] + cross[bands:, 0:bands] + cross[bands:, bands:]
    side = jnp.zeros((bands, 2 * bands), jnp.float32)
    for kind in range(KINDS):
        high, low = split(crossed[kind] * own_edges)
        side = side + (dot(windows[kind], high, NT) + dot(windows[kind], low, NT))
    eye = (
        lax.broadcasted_iota(jnp.int32, (bands, bands), 0) == lax.broadcasted_iota(jnp.int32, (bands, bands), 1)
    ).astype(jnp.float32)
    flipped = exact(eye, total, NT) - side[:, 0:bands] - side[:, bands:]
    flipped = flipped * (1.0 / (4 * groups * window))

    everyone = groups * owners
    span = tile_rows * band_share
    lanes = owners * span
    source = lax.broadcasted_iota(jnp.int32, (bands, lanes), 0)
    lane_ids = lax.broadcasted_iota(jnp.int32, (bands, lanes), 1)
    wanted = lane_ids // span * band_share + lane_ids % band_share
    repeated = exact(flipped, (source == wanted).astype(jnp.float32), NN)
    kept = jnp.where(source % tile_rows == lane_ids % span // band_share, repeated, 0.0)
    gather = lax.broadcasted_iota(jnp.int32, (groups, bands), 1) // tile_rows == lax.broadcasted_iota(
        jnp.int32, (groups, bands), 0)
    packed = exact(gather.astype(jnp.float32), kept, NN)
    for z in range(owners):
        for g in range(groups):
            tiles[z * groups + g] = packed[g:g + 1, z * span:(z + 1) * span]
    here = level * groups + me
    landed[pl.ds(here, 1)] = tiles[pl.ds(here, 1)]
    pl.semaphore_wait(ready, groups - 1)
    outgoing = []
    for d in range(1, everyone):
        peer = (here + d) % everyone
        copy = pltpu.make_async_remote_copy(
            src_ref=tiles.at[peer], dst_ref=landed.at[here], send_sem=fin_send.at[peer], recv_sem=fin_recv.at[here],
            device_id=(peer % groups, peer // groups), device_id_type=MESH,
        )
        copy.start()
        outgoing.append(copy)
    for d in range(1, everyone):
        peer = (here + d) % everyone
        pltpu.make_async_remote_copy(
            src_ref=tiles.at[peer], dst_ref=landed.at[peer], send_sem=fin_send.at[peer], recv_sem=fin_recv.at[peer],
            device_id=(peer % groups, peer // groups), device_id_type=MESH,
        ).wait_recv()
    row_ids = lax.broadcasted_iota(jnp.int32, (tile_rows, span), 0)
    keep = row_ids == lax.broadcasted_iota(jnp.int32, (tile_rows, span), 1) // band_share
    pick = lax.broadcasted_iota(jnp.int32, (span, band_share), 0) % band_share == lax.broadcasted_iota(
        jnp.int32, (span, band_share), 1)
    for h in range(2):
        row = jnp.sum(landed[h * everyone // 2:(h + 1) * everyone // 2], axis=0)
        out_ref[h] = exact(jnp.where(keep, row, 0.0), pick.astype(jnp.float32), NN)

    for copy in outgoing:
        copy.wait_send()
    for q in range(CHUNKS):
        to_far[q].wait_send()
        near_direct[q].wait_send()
        far_on[q].wait_send()
        near_on[q].wait_send()
    to_sibling.wait_send()
    to_turn.wait_send()


def solution(mesh):
    groups, owners = mesh.shape["bl"], mesh.shape["bp"]

    def body(inverse_cov, channel_keep_mask, partner_ids, band_starts):
        count, rows, channels = inverse_cov.shape
        width, bands = channels // 2, band_starts.shape[1]
        assert count == 1 and groups % 4 == 0 and width == 2 * rows
        f32, bf16 = jnp.float32, jnp.bfloat16
        block = pltpu.VMEM((rows, width), f32)
        tile_rows = bands // groups
        dma = pltpu.SemaphoreType.DMA
        vmem = pl.BlockSpec(memory_space=pltpu.VMEM)
        found = pl.pallas_call(
            partial(kernel, (groups, owners, rows, width, bands)),
            name="fisher",
            out_shape=jax.ShapeDtypeStruct((2, tile_rows, bands // owners), f32),
            in_specs=[pl.BlockSpec(memory_space=pltpu.HBM)] * 4,
            out_specs=vmem,
            scratch_shapes=[
                block,
                pltpu.VMEM(channel_keep_mask.shape, jnp.int32),
                pltpu.VMEM(partner_ids.shape, jnp.int32),
                pltpu.VMEM(band_starts.shape, jnp.int32),
                block,
                pltpu.VMEM((rows, rows), f32),
                block, block, block, block, block,
                pltpu.VMEM((KINDS, rows, rows), bf16),
                pltpu.VMEM((KINDS, rows, rows), bf16),
                pltpu.VMEM((KINDS, rows, width), f32),
                pltpu.VMEM((KINDS, rows, 2 * bands), f32),
                pltpu.VMEM((KINDS + 1, bands, width), bf16),
                pltpu.VMEM((2 * bands, width), f32),
                pltpu.VMEM((2 * bands + 2 * KINDS, width), f32),
                pltpu.VMEM((2 * bands + 2 * KINDS, width), f32),
                pltpu.VMEM((KINDS, 2 * bands, width), f32),
                pltpu.VMEM((groups * owners, 1, tile_rows * bands // owners), f32),
                pltpu.VMEM((groups * owners, 1, tile_rows * bands // owners), f32),
                dma((4,)), dma((2, 1)), dma((2, 1)),
                dma((2, CHUNKS)), dma((2, CHUNKS)), dma((2, CHUNKS)), dma((2, CHUNKS)),
                dma((groups * owners,)), dma((groups * owners,)), pltpu.SemaphoreType.REGULAR,
            ],
            compiler_params=pltpu.CompilerParams(
                collective_id=0, has_side_effects=True, vmem_limit_bytes=67043328
            ),
        )(inverse_cov, channel_keep_mask, partner_ids, band_starts)
        return jnp.swapaxes(found, 1, 2)

    placed = (P("bl", "bp", None), P("bl", None), P("bl", None), P())
    return jax.shard_map(body, mesh=mesh, in_specs=placed, out_specs=P(None, "bp", "bl"), check_vma=False)
```

profile of v0, /device:TPU:0, one launch (start us, length us, event | category | flops | bytes accessed | tf_op | source)
XLA Modules:
  0.0 36.1 jit_solution(4842643945277608470)
XLA Ops:
  0.0 34.8 %fisher.1 = f32[2,8,16]{2,1,0:T(8,128)} custom-call(f32[1,256,1024]{2,1,0:T(8,128)} %cov_ref.1, s32[1,1024]{1,0:T(1,128)} %mask_ref.1, s32[1,2]{1,0:T(1,128)} %partner_ref.1, s32[2,64]{1,0:T(2,128)} %starts_ref.1), custom_call_target="tpu_custom_call" | custom-call | tf_op jit(solution)/shard_map/fisher/pallas_call | solution.py:337
  34.8 1.3 %copy.6 = f32[2,16,8]{1,2,0:T(8,128)} copy(f32[2,16,8]{1,2,0:T(8,128)} %bitcast.1) | data formatting | bytes 2048
where the time goes:
time: 36.3 us; the launch traced here: 36.1 us
  Pallas kernels  34.8 us (96%)
  local copies, waits for them, and re-layouts  1.3 us (4%)
    pallas_call x1, Pallas kernels, body(): pl.pallas_call(partial(kernel, (groups, owners, rows, width, bands)), nam...  34.8 us
    unnamed x1, local copies, waits for them, and re-layouts  1.3 us

commit v1 on v0

v1 whole, which is shorter than its diff:
```python
from functools import partial

import jax
import jax.numpy as jnp
from jax import lax
from jax.experimental import pallas as pl
from jax.experimental.pallas import tpu as pltpu
from jax.sharding import PartitionSpec as P

WINDOW_LENGTH = 128
KINDS = 4
LANES = 128
PAD = 8
MESH = pl.DeviceIdType.MESH
NT = (((1,), (1,)), ((), ()))
NN = (((1,), (0,)), ((), ()))
F32, BF16 = jnp.float32, jnp.bfloat16


def split(value):
    high = value.astype(BF16)
    return high, (value - high.astype(F32)).astype(BF16)


def dot(left, right, dims):
    return lax.dot_general(left, right, dims, preferred_element_type=F32)


def dot3(left, right, dims):
    return dot(left[0], right[0], dims) + (dot(left[0], right[1], dims) + dot(left[1], right[0], dims))


def exact(left, right, dims):
    return lax.dot_general(left, right, dims, precision=lax.Precision.HIGHEST, preferred_element_type=F32)


def iota(shape, axis):
    return lax.broadcasted_iota(jnp.int32, shape, axis)


def column_of(row, length, offset):
    shape = (length, row.shape[1])
    spot = iota(shape, 0) + offset == iota(shape, 1)
    return jnp.sum(jnp.where(spot, row, 0.0), axis=1, keepdims=True)


def decay(gap, inverse_length):
    return jnp.exp(-jnp.abs(gap) * inverse_length)


def inverse_of(ids):
    return 1.0 / (1.0 + (ids % KINDS).astype(F32))


def flipped(index, distance):
    result, bit = index, 1
    while bit <= distance:
        if distance & bit:
            result = result + bit - 2 * bit * (index // bit % 2)
        bit *= 2
    return result


def kernel(
    sizes, cov_ref, mask_ref, partner_ref, starts_ref, out_ref,
    raw, masks, partner_row, starts,
    slices, mask_all, partner_all, rim, tail, rim_out, tail_out,
    toep, toep_low, table, table_low, spread, spread_low, box, pick, reach,
    held, boxed, leak, mixed, grown, product, tiles, landed,
    load_sem, x_sem, m_sem, p_sem, c_sem, w_sem, fin_send, fin_recv, ready,
):
    groups, owners, rows, width, bands, seats = sizes
    window = WINDOW_LENGTH
    me, level = lax.axis_index("bl"), lax.axis_index("bp")
    per_half = width // rows
    half, place = level // per_half, level % per_half
    level_other = half * per_half + (per_half - 1 - place)
    slots = per_half * groups
    count = rows // groups
    share = bands // slots
    slot = place * groups + me
    first = pl.multiple_of(place * rows, rows)
    mine = pl.ds(first, rows)
    half_columns = pl.ds(pl.multiple_of(half * width, width), width)

    starts_load = pltpu.make_async_copy(starts_ref, starts, load_sem.at[2])
    loads = [
        pltpu.make_async_copy(cov_ref.at[0, :, half_columns], raw, load_sem.at[0]),
        pltpu.make_async_copy(mask_ref, masks, load_sem.at[1]),
        pltpu.make_async_copy(partner_ref, partner_row, load_sem.at[3]),
    ]
    for load in loads:
        load.start()
    starts_load.start()
    barrier = pltpu.get_barrier_semaphore()
    for d in range(1, groups):
        pl.semaphore_signal(barrier, inc=1, device_id=(flipped(me, d), level), device_id_type=MESH)
    for d in range(1, owners):
        pl.semaphore_signal(barrier, inc=1, device_id=(me, (level + d) % owners), device_id_type=MESH)
    for load in loads:
        load.wait()
    pl.semaphore_wait(barrier, groups + owners - 2)

    def remote(source, target, sems, to, origin, device):
        return pltpu.make_async_remote_copy(
            src_ref=source, dst_ref=target, send_sem=sems.at[0, to], recv_sem=sems.at[1, origin],
            device_id=device, device_id_type=MESH,
        )

    def slice_of(g):
        return raw.at[pl.ds(pl.multiple_of(g * count, count), count)]

    order = list(range(1, groups))
    sent = []
    for d in order:
        g = flipped(me, d)
        sent.append(remote(masks, mask_all.at[me], m_sem, g, me, (g, level)))
        sent.append(remote(partner_row, partner_all.at[me], p_sem, g, me, (g, level)))
    for d in order:
        g = flipped(me, d)
        sent.append(remote(slice_of(g), slices.at[me], x_sem, g, me, (g, level)))
    for copy in sent:
        copy.start()
    for d in order:
        pl.semaphore_signal(ready, inc=1, device_id=(flipped(me, d), level), device_id_type=MESH)
    slices[me] = raw[pl.ds(pl.multiple_of(me * count, count), count), :]
    mask_all[me] = masks[...]
    partner_all[me] = partner_row[...]

    starts_load.wait()
    start_row = starts[pl.ds(half, 1), :].astype(F32)
    start = column_of(start_row, bands, 0)
    band_ids = iota((bands, 1), 0)
    inverse_length = inverse_of(band_ids)
    channel = iota((bands, width), 1).astype(F32)
    ahead = channel - start
    past = ahead - (window - 1)
    within = jnp.logical_and(ahead >= 0.0, past <= 0.0)
    rise, fall = decay(ahead, inverse_length), decay(past, inverse_length)
    ramp_rise = jnp.where(within, rise, 0.0)
    ramp_fall = jnp.where(within, fall, 0.0)
    edge_up = jnp.where(ahead < 0.0, rise, 0.0)
    edge_down = jnp.where(past > 0.0, fall, 0.0)
    mid_ids = iota((2 * KINDS, 1), 0)
    mid_channel = iota((2 * KINDS, width), 1).astype(F32) - rows
    mid_gap = jnp.where(mid_ids < KINDS, -1.0 - mid_channel, mid_channel)
    edge_mid = jnp.where(mid_gap >= 0.0, decay(mid_gap, inverse_of(mid_ids)), 0.0)
    fence_ids = iota((slots * KINDS, 1), 0)
    fence_gap = (fence_ids // KINDS * count - 1).astype(F32) - iota((slots * KINDS, width), 1).astype(F32)
    fence = jnp.where(fence_gap >= 0.0, decay(fence_gap, inverse_of(fence_ids)), 0.0)
    table[...], table_low[...] = split(
        jnp.concatenate([edge_up, edge_down, edge_mid, jnp.zeros_like(edge_mid), ramp_rise, ramp_fall], axis=0))
    ramp_at = 2 * bands + 4 * KINDS

    marks = masks[:, half_columns].astype(F32)
    panel = split(raw[...] * column_of(marks, rows, first) * marks)
    summed = dot3(split(jnp.concatenate([fence, edge_up, ramp_rise], axis=0)), panel, NT)
    fences, ups, rises = summed[:slots * KINDS], summed[slots * KINDS:slots * KINDS + bands], summed[slots * KINDS + bands:]
    rim_out[...] = jnp.zeros_like(rim_out)
    for s in range(slots):
        rim_out[s, 0:KINDS, :] = fences[s * KINDS:(s + 1) * KINDS]
        rim_out[s, KINDS:KINDS + share, :] = ups[s * share:(s + 1) * share]
        tail_out[s] = rises[s * share:(s + 1) * share]
    rim[me, :, mine] = rim_out[slot]
    tail[me, :, mine] = tail_out[slot]
    pl.semaphore_wait(ready, groups - 1)
    origin = place * groups + me

    def rim_copies(d, far):
        g = flipped(me, d)
        where, row = (level_other, per_half - 1 - place) if far else (level, place)
        to = row * groups + g
        return [
            remote(rim_out.at[to], rim.at[me, :, mine], c_sem, to, origin, (g, where)),
            remote(tail_out.at[to], tail.at[me, :, mine], w_sem, to, origin, (g, where)),
        ]

    rims = [rim_copies(d, far) for d in range(groups) for far in (False, True) if far or d]
    for kind in range(2):
        for pair in rims:
            pair[kind].start()
            sent.append(pair[kind])

    far_apart = (iota((rows, rows), 0) - iota((rows, rows), 1)).astype(F32)
    for k in range(KINDS):
        toep[k], toep_low[k] = split(decay(far_apart, 1.0 / (1 + k)))
    for k in range(KINDS):
        box[:, k * width:(k + 1) * width] = jnp.where(
            jnp.logical_and(within, band_ids % KINDS == k), 1.0, 0.0).astype(BF16)
    sides = iota((bands, 2 * bands), 1) % bands == iota((bands, 2 * bands), 0)
    box[:, KINDS * width:] = jnp.where(sides, -1.0, 0.0).astype(BF16)

    tile_b, tile_a = bands // groups, bands // owners
    span = tile_a * tile_b
    lanes = owners * span
    lane_band = iota((bands, lanes), 1) // tile_b
    lane_start = exact(start_row, (lane_band == iota((bands, lanes), 0)).astype(F32), NN)
    step_rows = KINDS * count
    row_ids = iota((step_rows, lanes), 0)
    row_channel = (row_ids % count + slot * count).astype(F32)
    row_ahead = row_channel - lane_start
    inside = jnp.logical_and(row_ahead >= 0.0, row_ahead <= window - 1.0)
    of_kind = iota((step_rows, lanes), 1) // tile_b % KINDS == row_ids // count
    pick[0:step_rows, :] = jnp.where(jnp.logical_and(inside, of_kind), 1.0, 0.0)
    rim_band = slot * share + iota((PAD, lanes), 0) - KINDS
    own_band = jnp.logical_and(iota((PAD, lanes), 1) // tile_b == rim_band, iota((PAD, lanes), 0) >= KINDS)
    pick[step_rows:, :] = jnp.where(
        jnp.logical_and(own_band, iota((PAD, lanes), 0) < KINDS + share), -1.0, 0.0)

    total = groups * count
    gap = (iota((step_rows, total), 0) % count - iota((step_rows, total), 1) % count).astype(F32)
    reach_value = decay(gap, inverse_of(iota((step_rows, total), 0) // count))
    reach[...] = jnp.where(gap > 0.0, reach_value, jnp.where(gap == 0.0, 0.5, 0.0))

    def wait_from(target, sems, origin_index, device):
        remote(target, target, sems, origin_index, origin_index, device).wait_recv()

    for d in order:
        g = flipped(me, d)
        wait_from(partner_all.at[g], p_sem, g, (g, level))
        wait_from(mask_all.at[g], m_sem, g, (g, level))

    lane_of = iota((1, total), 1) // count
    lane_pad = iota((1, groups * PAD), 1) // PAD
    seat_lane, seat_pad, seat_value = [], [], []
    for k in range(seats):
        values = [partner_all[i][:, k:k + 1] for i in range(groups)]
        seat_value.append(values)
        seat_lane.append(sum(jnp.where(lane_of == i, values[i], 0) for i in range(groups)))
        seat_pad.append(sum(jnp.where(lane_pad == i, values[i], 0) for i in range(groups)))

    def weights(j, ids, by_lane):
        found = 0.0
        for k in range(seats):
            found = found + jnp.where(ids == seat_value[k][j], 1.0, 0.0) + jnp.where(by_lane[k] == j, 1.0, 0.0)
        return found

    blend_rows = []
    slot_lane = iota((PAD, groups * PAD), 1) % PAD == iota((PAD, groups * PAD), 0)
    for j in range(groups):
        spread[j], spread_low[j] = split(reach[...] * weights(j, lane_of, seat_lane))
        blend_rows.append(jnp.where(slot_lane, weights(j, lane_pad, seat_pad), 0.0))
    blend = jnp.concatenate(blend_rows, axis=0).astype(BF16)

    lane_f = iota((1, rows), 1).astype(F32)

    def filtered(value):
        n = value.shape[0]
        found = dot3(split(value), (table[0:ramp_at, :], table_low[0:ramp_at, :]), NT)
        stacked = split(jnp.concatenate([value[:, 0:rows], value[:, rows:]], axis=0))
        both = jnp.concatenate(stacked, axis=0)
        results = []
        for k in range(KINDS):
            r = dot(both, toep[k], NN)
            r = r[0:2 * n] + r[2 * n:] + dot(stacked[0], toep_low[k], NN)
            up = found[:, 2 * bands + k:2 * bands + k + 1]
            down = found[:, 2 * bands + KINDS + k:2 * bands + KINDS + k + 1]
            left = r[0:n] + down * jnp.exp((rows - lane_f) * (-1.0 / (1 + k)))
            right = r[n:] + up * jnp.exp((lane_f + 1.0) * (-1.0 / (1 + k)))
            results.append((left, right))
        return found[:, 0:2 * bands], results

    def ramped(value):
        return dot3(split(value), (table[ramp_at:, :], table_low[ramp_at:, :]), NT)

    in_lane = slot * count
    lane_base = pl.multiple_of(half * width + in_lane // LANES * LANES, LANES)
    lane_offset = in_lane % LANES

    def absorb(j):
        column_marks = mask_all[j, :, half_columns].astype(F32)
        near_marks = mask_all[j, :, pl.ds(lane_base, LANES)].astype(F32)
        value = slices[j] * column_of(near_marks, count, lane_offset) * column_marks
        held[j, :, 0:width] = value
        edges, results = filtered(value)
        leak[j] = edges
        for k in range(KINDS):
            boxed[k, j, :, 0:rows] = results[k][0]
            boxed[k, j, :, rows:] = results[k][1]
        held[j, :, width:] = ramped(value)

    absorb(me)
    for d in order:
        g = flipped(me, d)
        wait_from(slices.at[g], x_sem, g, (g, level))
        absorb(g)

    for d in range(groups):
        g = flipped(me, d)
        if d:
            wait_from(rim.at[g, :, mine], c_sem, place * groups + g, (g, level))
        other = pl.ds(pl.multiple_of(width - rows - first, rows), rows)
        wait_from(rim.at[g, :, other], c_sem, (per_half - 1 - place) * groups + g, (g, level_other))
    rims_in = jnp.reshape(rim[...], (groups * PAD, width))
    rims_in = jnp.concatenate([rims_in, ramped(rims_in)], axis=1)
    high, low = split(rims_in)
    mixed[...] = dot(blend, high, NN) + dot(blend, low, NN)

    held_split = split(jnp.reshape(held[...], (total, width + 2 * bands)))
    rank = (iota((count, 1), 0) + 1).astype(F32)
    for j in range(groups):
        found = dot3((spread[j], spread_low[j]), held_split, NN)
        for m in range(KINDS):
            at = slice(m * count, (m + 1) * count)
            carry = mixed[j * PAD + m:j * PAD + m + 1, :]
            grown[j, at, :] = found[at] + jnp.exp(rank * (-1.0 / (1 + m))) * carry

    for d in range(groups):
        g = flipped(me, d)
        if d:
            wait_from(tail.at[g, :, mine], w_sem, place * groups + g, (g, level))
        other = pl.ds(pl.multiple_of(width - rows - first, rows), rows)
        wait_from(tail.at[g, :, other], w_sem, (per_half - 1 - place) * groups + g, (g, level_other))
    blank, spare = jnp.zeros((KINDS, width), F32), jnp.zeros((KINDS - share, width), F32)
    tails = []
    for j in range(groups):
        tails += [blank, tail[j]] + ([spare] if share < KINDS else [])
    tail_edges, tail_results = filtered(jnp.concatenate(tails, axis=0))

    for k in range(KINDS):
        line = jnp.concatenate(tail_results[k], axis=1)
        product[step_rows:, k * width:(k + 1) * width] = sum(
            mixed[j * PAD:(j + 1) * PAD, 0:width] * line[j * PAD:(j + 1) * PAD] for j in range(groups))
    product[step_rows:, KINDS * width:] = sum(
        mixed[j * PAD:(j + 1) * PAD, width:] * tail_edges[j * PAD:(j + 1) * PAD] for j in range(groups))

    for pb in range(count // 8):
        here = slice(pb * 8, pb * 8 + 8)
        for m in range(KINDS):
            rows_at = slice(m * count + pb * 8, m * count + pb * 8 + 8)
            product[rows_at, KINDS * width:] = sum(
                grown[j, rows_at, width:] * leak[j, here, :] for j in range(groups))
        for qb in range(width // LANES):
            cols = slice(qb * LANES, (qb + 1) * LANES)
            sums = [[0.0] * KINDS for _ in range(KINDS)]
            for j in range(groups):
                lefts = [grown[j, m * count + pb * 8:m * count + pb * 8 + 8, cols] for m in range(KINDS)]
                rights = [boxed[k, j, here, cols] for k in range(KINDS)]
                for m in range(KINDS):
                    for k in range(KINDS):
                        term = lefts[m] * rights[k]
                        sums[m][k] = term if j == 0 else sums[m][k] + term
            for m in range(KINDS):
                for k in range(KINDS):
                    product[m * count + pb * 8:m * count + pb * 8 + 8,
                            k * width + qb * LANES:k * width + (qb + 1) * LANES] = sums[m][k]

    high, low = split(product[...])
    turned = split(dot(box[...], high, NT) + dot(box[...], low, NT))
    picks = pick[...].astype(BF16)
    fisher = (dot(turned[0], picks, NN) + dot(turned[1], picks, NN)) * (1.0 / (4 * groups * window))
    kept = jnp.where(iota((bands, lanes), 0) % tile_b == iota((bands, lanes), 1) % tile_b, fisher, 0.0)
    for g in range(groups):
        packed = jnp.sum(kept[g * tile_b:(g + 1) * tile_b], axis=0, keepdims=True)
        for z in range(owners):
            tiles[z * groups + g] = packed[:, z * span:(z + 1) * span]

    everyone = groups * owners
    here = level * groups + me
    landed[pl.ds(here, 1)] = tiles[pl.ds(here, 1)]
    for d in range(1, everyone):
        peer = (here + d) % everyone
        copy = pltpu.make_async_remote_copy(
            src_ref=tiles.at[peer], dst_ref=landed.at[here], send_sem=fin_send.at[peer], recv_sem=fin_recv.at[here],
            device_id=(peer % groups, peer // groups), device_id_type=MESH,
        )
        copy.start()
        sent.append(copy)
    for d in range(1, everyone):
        peer = (here + d) % everyone
        pltpu.make_async_remote_copy(
            src_ref=tiles.at[peer], dst_ref=landed.at[peer], send_sem=fin_send.at[peer], recv_sem=fin_recv.at[peer],
            device_id=(peer % groups, peer // groups), device_id_type=MESH,
        ).wait_recv()
    keep = iota((tile_a, span), 0) == iota((tile_a, span), 1) // tile_b
    spots = (iota((span, tile_b), 0) % tile_b == iota((span, tile_b), 1)).astype(F32)
    for h in range(2):
        row = jnp.sum(landed[h * everyone // 2:(h + 1) * everyone // 2], axis=0)
        out_ref[h] = exact(jnp.where(keep, row, 0.0), spots, NN)
    for copy in sent:
        copy.wait_send()


def solution(mesh):
    groups, owners = mesh.shape["bl"], mesh.shape["bp"]

    def body(inverse_cov, channel_keep_mask, partner_ids, band_starts):
        number, rows, channels = inverse_cov.shape
        width, bands, seats = channels // 2, band_starts.shape[1], partner_ids.shape[1]
        per_half = width // rows
        slots = per_half * groups
        count, share = rows // groups, bands // slots
        assert number == 1 and per_half == 2 and count % 8 == 0 and 1 <= share <= KINDS
        tile_b, tile_a = bands // groups, bands // owners
        wide = width + 2 * bands
        step_rows = KINDS * count
        everyone = groups * owners
        dma = pltpu.SemaphoreType.DMA

        def vmem(shape, dtype=F32):
            return pltpu.VMEM(shape, dtype)

        return pl.pallas_call(
            partial(kernel, (groups, owners, rows, width, bands, seats)),
            name="fisher",
            out_shape=jax.ShapeDtypeStruct((2, tile_a, tile_b), F32),
            in_specs=[pl.BlockSpec(memory_space=pltpu.HBM)] * 4,
            out_specs=pl.BlockSpec(memory_space=pltpu.VMEM),
            scratch_shapes=[
                vmem((rows, width)),
                vmem(channel_keep_mask.shape, jnp.int32),
                vmem(partner_ids.shape, jnp.int32),
                vmem(band_starts.shape, jnp.int32),
                vmem((groups, count, width)),
                vmem((groups, 1, channels), jnp.int32),
                vmem((groups, 1, seats), jnp.int32),
                vmem((groups, PAD, width)),
                vmem((groups, share, width)),
                vmem((slots, PAD, rows)),
                vmem((slots, share, rows)),
                vmem((KINDS, rows, rows), BF16),
                vmem((KINDS, rows, rows), BF16),
                vmem((4 * bands + 4 * KINDS, width), BF16),
                vmem((4 * bands + 4 * KINDS, width), BF16),
                vmem((groups, step_rows, rows), BF16),
                vmem((groups, step_rows, rows), BF16),
                vmem((bands, KINDS * width + 2 * bands), BF16),
                vmem((step_rows + PAD, bands * tile_b)),
                vmem((step_rows, rows)),
                vmem((groups, count, wide)),
                vmem((KINDS, groups, count, width)),
                vmem((groups, count, 2 * bands)),
                vmem((groups * PAD, wide)),
                vmem((groups, step_rows, wide)),
                vmem((step_rows + PAD, KINDS * width + 2 * bands)),
                vmem((everyone, 1, tile_a * tile_b)),
                vmem((everyone, 1, tile_a * tile_b)),
                dma((4,)), dma((2, groups)), dma((2, groups)), dma((2, groups)), dma((2, slots)), dma((2, slots)),
                dma((everyone,)), dma((everyone,)), pltpu.SemaphoreType.REGULAR,
            ],
            compiler_params=pltpu.CompilerParams(
                collective_id=0, has_side_effects=True, vmem_limit_bytes=67043328
            ),
        )(inverse_cov, channel_keep_mask, partner_ids, band_starts)

    placed = (P("bl", "bp", None), P("bl", None), P("bl", None), P())
    return jax.shard_map(body, mesh=mesh, in_specs=placed, out_specs=P(None, "bp", "bl"), check_vma=False)
```

time: 36.3 us -> 28.9 us (0.80)
  Pallas kernels: 34.8 us -> 27.2 us
    pallas_call x1, Pallas kernels: 34.8 us -> 27.2 us  [body(): pl.pallas_call(partial(kernel, (groups, owners, rows, width, bands, seats...]
    pallas_call x0 -> x1, local copies, waits for them, and re-layouts: none -> 1.38 us  [body(): pl.pallas_call(partial(kernel, (groups, owners, rows, width, bands, seats...]
    unnamed x1 -> x0, local copies, waits for them, and re-layouts: 1.3 us -> none
where the time goes in v1:
time: 28.9 us; the launch traced here: 28.6 us
  Pallas kernels  27.2 us (94%)
  local copies, waits for them, and re-layouts  1.38 us (5%)
    pallas_call x1, Pallas kernels, body(): pl.pallas_call(partial(kernel, (groups, owners, rows, width, bands, seats...  27.2 us
    pallas_call x1, local copies, waits for them, and re-layouts, body(): pl.pallas_call(partial(kernel, (groups, owners, rows, width, bands, seats...  1.38 us

profile of v1, /device:TPU:0, one launch (start us, length us, event | category | flops | bytes accessed | tf_op | source)
XLA Modules:
  0.0 28.6 jit_solution(3479637466565317526)
XLA Ops:
  0.0 27.2 %fisher.1 = f32[2,16,8]{2,1,0:T(8,128)} custom-call(f32[1,256,1024]{2,1,0:T(8,128)} %cov_ref.1, s32[1,1024]{1,0:T(1,128)} %mask_ref.1, s32[1,2]{1,0:T(1,128)} %partner_ref.1, s32[2,64]{1,0:T(2,128)} %starts_ref.1), custom_call_target="tpu_custom_call" | custom-call | tf_op jit(solution)/shard_map/fisher/pallas_call | solution.py:403
  27.3 1.4 %copy.5 = f32[2,16,8]{1,2,0:T(8,128)} copy(f32[2,16,8]{2,1,0:T(8,128)} %fisher.1) | data formatting | bytes 2048 | tf_op jit(solution)/shard_map/fisher/pallas_call | solution.py:403

commit v2 on v1

v2 whole, which is shorter than its diff:
```python
from functools import partial

import jax
import jax.numpy as jnp
from jax import lax
from jax.experimental import pallas as pl
from jax.experimental.pallas import tpu as pltpu
from jax.sharding import PartitionSpec as P

WINDOW_LENGTH = 128
KINDS = 4
LANES = 128
PAD = 8
LATE = 2
MESH = pl.DeviceIdType.MESH
NT = (((1,), (1,)), ((), ()))
NN = (((1,), (0,)), ((), ()))
F32, BF16 = jnp.float32, jnp.bfloat16


def split(value):
    high = value.astype(BF16)
    return high, (value - high.astype(F32)).astype(BF16)


def dot(left, right, dims):
    return lax.dot_general(left, right, dims, preferred_element_type=F32)


def dot3(left, right, dims):
    return dot(left[0], right[0], dims) + (dot(left[0], right[1], dims) + dot(left[1], right[0], dims))


def exact(left, right, dims):
    return lax.dot_general(left, right, dims, precision=lax.Precision.HIGHEST, preferred_element_type=F32)


def iota(shape, axis):
    return lax.broadcasted_iota(jnp.int32, shape, axis)


def column_of(row, length, offset):
    shape = (length, row.shape[1])
    spot = iota(shape, 0) + offset == iota(shape, 1)
    return jnp.sum(jnp.where(spot, row, 0.0), axis=1, keepdims=True)


def decay(gap, inverse_length):
    return jnp.exp(-jnp.abs(gap) * inverse_length)


def inverse_of(ids):
    return 1.0 / (1.0 + (ids % KINDS).astype(F32))


def flipped(index, distance):
    result, bit = index, 1
    while bit <= distance:
        if distance & bit:
            result = result + bit - 2 * bit * (index // bit % 2)
        bit *= 2
    return result


def ordered(groups):
    bits = (groups // 2).bit_length() - 1
    far = [d for d in range(1, groups) if bin(d // 2).count("1") == bits]
    direct = [d for d in range(2, groups) if d not in far]
    late = direct[1::2] if len(direct) == 2 * LATE else direct[-LATE:]
    return [d for d in direct if d not in late], far, late


def kernel(
    sizes, cov_ref, mask_ref, partner_ref, starts_ref, out_ref,
    raw, masks, partner_row, starts,
    slices, mask_all, partner_all, rim, rim_out,
    toep, toep_low, table, table_low, spread, spread_low, box, pick,
    held, boxed, leak, blended, mixed, summits, grown, product, tiles, landed,
    load_sem, x_sem, m_sem, p_sem, c_sem, fin_sem, ready, ready_levels,
):
    groups, owners, rows, width, bands, seats = sizes
    window = WINDOW_LENGTH
    me, level = lax.axis_index("bl"), lax.axis_index("bp")
    per_half = width // rows
    half, place = level // per_half, level % per_half
    slots = per_half * groups
    count = rows // groups
    share = bands // slots
    slot = place * groups + me
    first = pl.multiple_of(place * rows, rows)
    mine = pl.ds(first, rows)
    other = pl.ds(pl.multiple_of(width - rows - first, rows), rows)
    half_columns = pl.ds(pl.multiple_of(half * width, width), width)
    early, far, late = ordered(groups)
    arrivals = [0, 1] + far + early + late
    seat_of = {d: n for n, d in enumerate(arrivals)}
    others = far + early + late + [1]
    fixed = groups - LATE
    peers = {d: flipped(me, d) for d in range(groups)}
    levels = {dz: flipped(level, dz) for dz in range(owners)}
    below, above = level > 0, level < owners - 1
    neighbours = below.astype(jnp.int32) + above.astype(jnp.int32)

    starts_load = pltpu.make_async_copy(starts_ref, starts, load_sem.at[2])
    loads = [
        pltpu.make_async_copy(cov_ref.at[0, :, half_columns], raw, load_sem.at[0]),
        pltpu.make_async_copy(mask_ref, masks, load_sem.at[1]),
        pltpu.make_async_copy(partner_ref, partner_row, load_sem.at[3]),
    ]
    starts_load.start()
    for load in loads:
        load.start()

    def tell(semaphore, device):
        pl.semaphore_signal(semaphore, inc=1, device_id=device, device_id_type=MESH)

    def tell_levels(semaphore):
        @pl.when(below)
        def _():
            tell(semaphore, (me, level - 1))

        @pl.when(above)
        def _():
            tell(semaphore, (me, level + 1))

    barrier = pltpu.get_barrier_semaphore()
    for d in others:
        tell(barrier, (peers[d], level))
    tell_levels(barrier)

    def remote(source, target, sems, n, device):
        return pltpu.make_async_remote_copy(
            src_ref=source, dst_ref=target, send_sem=sems.at[0, n], recv_sem=sems.at[1, n],
            device_id=device, device_id_type=MESH,
        )

    sent = []

    def send(copy):
        copy.start()
        sent.append(copy)

    def send_marks(d):
        n = seat_of[d]
        send(remote(partner_row, partner_all.at[n], p_sem, n, (peers[d], level)))
        send(remote(masks, mask_all.at[n], m_sem, n, (peers[d], level)))

    def send_slice(d):
        n, g = seat_of[d], peers[d]
        send(remote(raw.at[pl.ds(pl.multiple_of(g * count, count), count)], slices.at[n], x_sem, n, (g, level)))

    def send_rim(d, across):
        n, g = seat_of[d], peers[d]
        row = per_half - 1 - place if across else place
        send(remote(
            rim_out.at[row * groups + g], rim.at[n, :, mine], c_sem, across * groups + n, (g, levels[across])))

    def landing(target, sems, n, device):
        remote(target, target, sems, n, device).wait_recv()

    starts_load.wait()
    start_row = starts[pl.ds(half, 1), :].astype(F32)
    start = column_of(start_row, bands, 0)
    band_ids = iota((bands, 1), 0)
    inverse_length = inverse_of(band_ids)
    channel = iota((bands, width), 1).astype(F32)
    ahead = channel - start
    within = jnp.logical_and(ahead >= 0.0, ahead <= window - 1.0)
    rise = decay(ahead, inverse_length)
    fence_ids = iota((slots * KINDS, 1), 0)
    fence_gap = (fence_ids // KINDS * count - 1).astype(F32) - iota((slots * KINDS, width), 1).astype(F32)
    fence = jnp.where(fence_gap >= 0.0, decay(fence_gap, inverse_of(fence_ids)), 0.0)
    sources = split(jnp.concatenate(
        [fence, jnp.where(ahead < 0.0, rise, 0.0), jnp.where(within, rise, 0.0)], axis=0))

    for load in loads:
        load.wait()
    pl.semaphore_wait(barrier, groups - 1 + neighbours)
    tell_levels(ready_levels)
    for d in others:
        send_marks(d)
    for d in others:
        send_slice(d)
    slices[0] = raw[pl.ds(pl.multiple_of(me * count, count), count), :]
    mask_all[0] = masks[...]
    partner_all[0] = partner_row[...]

    marks = masks[:, half_columns].astype(F32)
    panel = split(raw[...] * column_of(marks, rows, first) * marks)
    summed = dot3(sources, panel, NT)
    fences, ups, rises = summed[:slots * KINDS], summed[slots * KINDS:slots * KINDS + bands], summed[slots * KINDS + bands:]
    if share < KINDS:
        rim_out[...] = jnp.zeros_like(rim_out)
    for s in range(slots):
        rim_out[s, 0:KINDS, :] = fences[s * KINDS:(s + 1) * KINDS]
        rim_out[s, KINDS:KINDS + share, :] = ups[s * share:(s + 1) * share]
        rim_out[s, PAD:PAD + share, :] = rises[s * share:(s + 1) * share]
    rim[0, :, mine] = rim_out[slot]
    def ladder(shape, axis):
        return iota(shape, axis).astype(F32)

    twice = jnp.concatenate([start_row, start_row], axis=1)
    pair_ids = iota((1, 2 * bands), 1)
    is_second = iota((width, 2 * bands), 1) >= bands
    pair_inverse = inverse_of(pair_ids)
    climb = ladder((width, 2 * bands), 0) - twice
    drop = climb - (window - 1.0)
    gap = jnp.where(is_second, drop, climb)
    fade = decay(gap, pair_inverse)
    inner = jnp.logical_and(climb >= 0.0, drop <= 0.0)
    outer = jnp.where(is_second, gap, -gap) > 0.0
    mid_ids = iota((1, LANES), 1)
    mid_channel = ladder((width, LANES), 0) - rows
    mid_lane = iota((width, LANES), 1)
    mid_gap = jnp.where(mid_lane < KINDS, -1.0 - mid_channel, mid_channel)
    mid_kept = jnp.logical_and(mid_gap >= 0.0, mid_lane < 2 * KINDS)
    table[...], table_low[...] = split(jnp.concatenate([
        jnp.where(outer, fade, 0.0), jnp.where(inner, fade, 0.0),
        jnp.where(mid_kept, decay(mid_gap, inverse_of(mid_ids)), 0.0)], axis=1))
    far_apart = (iota((rows, rows), 0) - iota((rows, rows), 1)).astype(F32)
    for k in range(KINDS):
        toep[k], toep_low[k] = split(decay(far_apart, 1.0 / (1 + k)))

    pl.semaphore_wait(ready_levels, neighbours)
    for d in range(1, groups):
        tell(ready, (peers[d], level))
    for d in others:
        send_rim(d, 0)

    lane_f = iota((1, rows), 1).astype(F32)
    wide = width + 2 * bands

    def filtered(value):
        n = value.shape[0]
        found = dot3(split(value), (table[...], table_low[...]), NN)
        stacked = split(jnp.concatenate([value[:, 0:rows], value[:, rows:]], axis=0))
        both = jnp.concatenate(stacked, axis=0)
        results = []
        for k in range(KINDS):
            r = dot(both, toep[k], NN)
            r = r[0:2 * n] + r[2 * n:] + dot(stacked[0], toep_low[k], NN)
            up = found[:, 4 * bands + k:4 * bands + k + 1]
            down = found[:, 4 * bands + KINDS + k:4 * bands + KINDS + k + 1]
            left = r[0:n] + down * jnp.exp((rows - lane_f) * (-1.0 / (1 + k)))
            right = r[n:] + up * jnp.exp((lane_f + 1.0) * (-1.0 / (1 + k)))
            results.append((left, right))
        return found[:, 0:2 * bands], found[:, 2 * bands:4 * bands], results

    in_lane = slot * count
    lane_base = pl.multiple_of(half * width + in_lane // LANES * LANES, LANES)
    lane_offset = in_lane % LANES

    def absorb(members):
        parts = []
        for n in members:
            near_marks = mask_all[n, :, pl.ds(lane_base, LANES)].astype(F32)
            part = slices[n] * column_of(near_marks, count, lane_offset) * mask_all[n, :, half_columns].astype(F32)
            held[n, :, 0:width] = part
            parts.append(part)
        edges, ramps, results = filtered(jnp.concatenate(parts, axis=0))
        for i, n in enumerate(members):
            at = slice(i * count, (i + 1) * count)
            leak[n] = edges[at]
            for k in range(KINDS):
                boxed[k, n, :, 0:rows] = results[k][0][at]
                boxed[k, n, :, rows:] = results[k][1][at]
            held[n, :, width:] = ramps[at]

    def take(n):
        device = (peers[arrivals[n]], level)
        landing(mask_all.at[n], m_sem, n, device)
        landing(slices.at[n], x_sem, n, device)

    take(1)
    absorb([0, 1])
    for k in range(KINDS):
        box[:, k * width:(k + 1) * width] = jnp.where(
            jnp.logical_and(within, band_ids % KINDS == k), 1.0, 0.0).astype(BF16)
    sides = iota((bands, 2 * bands), 1) % bands == iota((bands, 2 * bands), 0)
    box[:, KINDS * width:] = jnp.where(sides, -1.0, 0.0).astype(BF16)

    tile_b, tile_a = bands // groups, bands // owners
    span = tile_a * tile_b
    lanes = owners * span
    lane_band = iota((bands, lanes), 1) // tile_b
    lane_start = exact(start_row, (lane_band == iota((bands, lanes), 0)).astype(F32), NN)
    step_rows = KINDS * count
    row_ids = iota((step_rows, lanes), 0)
    row_ahead = (row_ids % count + slot * count).astype(F32) - lane_start
    inside = jnp.logical_and(row_ahead >= 0.0, row_ahead <= window - 1.0)
    of_kind = iota((step_rows, lanes), 1) // tile_b % KINDS == row_ids // count
    pick[0:step_rows, :] = jnp.where(jnp.logical_and(inside, of_kind), 1.0, 0.0)
    rim_row = iota((PAD, lanes), 0)
    own_band = jnp.logical_and(iota((PAD, lanes), 1) // tile_b == slot * share + rim_row - KINDS, rim_row >= KINDS)
    pick[step_rows:, :] = jnp.where(jnp.logical_and(own_band, rim_row < KINDS + share), -1.0, 0.0)

    pl.semaphore_wait(ready, groups - 1)
    for d in others + [0]:
        send_rim(d, 1)

    for n in range(1, groups):
        landing(partner_all.at[n], p_sem, n, (peers[arrivals[n]], level))
    names = [peers[d] for d in arrivals]
    total = fixed * count
    lane_of, lane_pad = iota((1, total), 1) // count, iota((1, groups * PAD), 1) // PAD
    chosen = [[partner_all[n][:, k:k + 1] for n in range(groups)] for k in range(seats)]

    def along(lane, values):
        found = jnp.zeros_like(lane)
        for n, value in enumerate(values):
            found = jnp.where(lane == n, value, found)
        return found

    named_lane, named_pad = along(lane_of, names[:fixed]), along(lane_pad, names)
    chosen_lane = [along(lane_of, chosen[k][:fixed]) for k in range(seats)]
    chosen_pad = [along(lane_pad, chosen[k]) for k in range(seats)]

    def weights(n, named, by_lane):
        found = 0.0
        for k in range(seats):
            found = found + jnp.where(named == chosen[k][n], 1.0, 0.0) + jnp.where(by_lane[k] == names[n], 1.0, 0.0)
        return found

    def weight(n, i):
        found = 0.0
        for k in range(seats):
            found = found + jnp.where(chosen[k][n] == names[i], 1.0, 0.0) + jnp.where(chosen[k][i] == names[n], 1.0, 0.0)
        return found

    step_gap = (iota((step_rows, total), 0) % count - iota((step_rows, total), 1) % count).astype(F32)
    reach = decay(step_gap, inverse_of(iota((step_rows, total), 0) // count))
    reach = jnp.where(step_gap > 0.0, reach, jnp.where(step_gap == 0.0, 0.5, 0.0))
    blend_rows = []
    pad_row = iota((PAD, groups * PAD), 0)
    slot_lane = jnp.logical_and(
        iota((PAD, groups * PAD), 1) % PAD == pad_row,
        jnp.logical_or(pad_row >= KINDS, iota((PAD, groups * PAD), 1) // PAD < fixed))
    for n in range(groups):
        spread[n], spread_low[n] = split(reach * weights(n, named_lane, chosen_lane))
        blend_rows.append(jnp.where(slot_lane, weights(n, named_pad, chosen_pad), 0.0))
    blend = jnp.concatenate(blend_rows, axis=0).astype(BF16)
    reach_one = split(reach[:, 0:count])

    for n in range(2, fixed, 2):
        for i in (n, n + 1):
            take(i)
        absorb([n, n + 1])

    held_split = split(jnp.reshape(held[0:fixed], (total, wide)))
    for n in range(groups):
        grown[n] = dot3((spread[n], spread_low[n]), held_split, NN)

    members = list(range(fixed, groups))
    for t in range(LATE):
        factors = [weight(fixed + t, n) for n in range(fixed)]
        leak[groups + t] = sum(factors[n] * leak[n] for n in range(fixed))
        for k in range(KINDS):
            blended[k, t] = sum(factors[n] * boxed[k, n] for n in range(fixed))
    for n in members:
        take(n)
    absorb(members)
    for t in range(LATE):
        n = fixed + t
        grown[groups + t] = dot3(reach_one, split(held[n]), NN)
        mutual = weight(n, fixed + 1 - t)
        leak[groups + t] = leak[groups + t] + mutual * leak[fixed + 1 - t]
        for k in range(KINDS):
            blended[k, t] = blended[k, t] + mutual * boxed[k, fixed + 1 - t]

    for copy in sent:
        copy.wait_send()
    sent.clear()
    for n in range(groups):
        d = arrivals[n]
        if d:
            landing(rim.at[n, :, mine], c_sem, n, (peers[d], level))
        landing(rim.at[n, :, other], c_sem, groups + n, (peers[d], levels[1]))
    blank = jnp.zeros((KINDS, width), F32)
    tops, tails = [], []
    for n in range(groups):
        tops.append(rim[n, 0:PAD, :])
        tails += [blank, rim[n, PAD:PAD + share, :]]
        if share < KINDS:
            tails.append(jnp.zeros((KINDS - share, width), F32))
    tops = jnp.concatenate(tops, axis=0)
    tail_edges, _, tail_results = filtered(jnp.concatenate(tails, axis=0))
    tops = jnp.concatenate([tops, dot3(split(tops), (table[:, 2 * bands:4 * bands], table_low[:, 2 * bands:4 * bands]), NN)], axis=1)
    summits[...] = tops
    high, low = split(tops)
    mixed[...] = dot(blend, high, NN) + dot(blend, low, NN)
    rank = (iota((count, 1), 0) + 1).astype(F32)
    fades = [jnp.exp(rank * (-1.0 / (1 + m))) for m in range(KINDS)]
    for k in range(KINDS):
        line = jnp.concatenate(tail_results[k], axis=1)
        product[step_rows:, k * width:(k + 1) * width] = sum(
            mixed[n * PAD:(n + 1) * PAD, 0:width] * line[n * PAD:(n + 1) * PAD] for n in range(groups))
    product[step_rows:, KINDS * width:] = sum(
        mixed[n * PAD:(n + 1) * PAD, width:] * tail_edges[n * PAD:(n + 1) * PAD] for n in range(groups))

    def gather(terms):
        for pb in range(count // 8):
            here = slice(pb * 8, pb * 8 + 8)
            spots = [slice(m * count + pb * 8, m * count + pb * 8 + 8) for m in range(KINDS)]
            for m in range(KINDS):
                found = sum((grown[n, spots[m], width:] + fades[m][here] * carry(m)[:, width:]) * edge[here, :] for n, edge, _, carry in terms)
                at = (spots[m], slice(KINDS * width, wide + (KINDS - 1) * width))
                product[at] = found
            for qb in range(width // LANES):
                cols = slice(qb * LANES, (qb + 1) * LANES)
                sums = [[None] * KINDS for _ in range(KINDS)]
                for n, _, box_ref, carry in terms:
                    lefts = [grown[n, spots[m], cols] + fades[m][here] * carry(m)[:, cols] for m in range(KINDS)]
                    rights = [box_ref(k)[here, cols] for k in range(KINDS)]
                    for m in range(KINDS):
                        for k in range(KINDS):
                            term = lefts[m] * rights[k]
                            sums[m][k] = term if sums[m][k] is None else sums[m][k] + term
                for m in range(KINDS):
                    for k in range(KINDS):
                        at = (spots[m], slice(k * width + qb * LANES, k * width + (qb + 1) * LANES))
                        product[at] = sums[m][k]

    def mixed_carry(n, m):
        return mixed.at[n * PAD + m:n * PAD + m + 1, :]

    def own_carry(n, m):
        return summits.at[n * PAD + m:n * PAD + m + 1, :]

    terms = [(n, leak.at[n], partial(lambda n, k: boxed.at[k, n], n), partial(mixed_carry, n)) for n in range(groups)]
    terms += [
        (groups + t, leak.at[groups + t], partial(lambda t, k: blended.at[k, t], t), partial(own_carry, fixed + t))
        for t in range(LATE)
    ]
    gather(terms)

    high, low = split(product[...])
    turned = split(dot(box[...], high, NT) + dot(box[...], low, NT))
    picks = pick[...].astype(BF16)
    fisher = (dot(turned[0], picks, NN) + dot(turned[1], picks, NN)) * (1.0 / (4 * groups * window))
    kept = jnp.where(iota((bands, lanes), 0) % tile_b == iota((bands, lanes), 1) % tile_b, fisher, 0.0)
    for g in range(groups):
        packed = jnp.sum(kept[g * tile_b:(g + 1) * tile_b], axis=0, keepdims=True)
        for z in range(owners):
            tiles[z * groups + g] = packed[:, z * span:(z + 1) * span]

    landed[0] = tiles[level * groups + me]
    finals = []
    for dz in reversed(range(owners)):
        for d in others + [0]:
            if dz or d:
                n = dz * groups + d
                copy = remote(tiles.at[levels[dz] * groups + peers[d]], landed.at[n], fin_sem, n, (peers[d], levels[dz]))
                send(copy)
                finals.append(copy)
    for copy in sent:
        copy.wait_send()
    for copy in finals:
        copy.wait_recv()
    for side in range(2):
        part = landed[side * per_half * groups:(side + 1) * per_half * groups]
        out_ref[pl.ds(half + side - 2 * side * half, 1), :] = jnp.sum(part, axis=0)


def solution(mesh):
    groups, owners = mesh.shape["bl"], mesh.shape["bp"]

    def body(inverse_cov, channel_keep_mask, partner_ids, band_starts):
        number, rows, channels = inverse_cov.shape
        width, bands, seats = channels // 2, band_starts.shape[1], partner_ids.shape[1]
        per_half = width // rows
        slots = per_half * groups
        count, share = rows // groups, bands // slots
        assert number == 1 and per_half == 2 and owners == 4 and count % 8 == 0 and 1 <= share <= KINDS
        tile_b, tile_a = bands // groups, bands // owners
        wide = width + 2 * bands
        step_rows = KINDS * count
        everyone = groups * owners
        dma = pltpu.SemaphoreType.DMA
        regular = pltpu.SemaphoreType.REGULAR

        def vmem(shape, dtype=F32):
            return pltpu.VMEM(shape, dtype)

        found = pl.pallas_call(
            partial(kernel, (groups, owners, rows, width, bands, seats)),
            name="fisher",
            out_shape=jax.ShapeDtypeStruct((2, tile_a * tile_b), F32),
            in_specs=[pl.BlockSpec(memory_space=pltpu.HBM)] * 4,
            out_specs=pl.BlockSpec(memory_space=pltpu.VMEM),
            scratch_shapes=[
                vmem((rows, width)),
                vmem(channel_keep_mask.shape, jnp.int32),
                vmem(partner_ids.shape, jnp.int32),
                vmem(band_starts.shape, jnp.int32),
                vmem((groups, count, width)),
                vmem((groups, 1, channels), jnp.int32),
                vmem((groups, 1, seats), jnp.int32),
                vmem((groups, PAD + share, width)),
                vmem((slots, PAD + share, rows)),
                vmem((KINDS, rows, rows), BF16),
                vmem((KINDS, rows, rows), BF16),
                vmem((width, 4 * bands + LANES), BF16),
                vmem((width, 4 * bands + LANES), BF16),
                vmem((groups, step_rows, (groups - LATE) * count), BF16),
                vmem((groups, step_rows, (groups - LATE) * count), BF16),
                vmem((bands, KINDS * width + 2 * bands), BF16),
                vmem((step_rows + PAD, bands * tile_b)),
                vmem((groups, count, wide)),
                vmem((KINDS, groups, count, width)),
                vmem((groups + LATE, count, 2 * bands)),
                vmem((KINDS, LATE, count, width)),
                vmem((groups * PAD, wide)),
                vmem((groups * PAD, wide)),
                vmem((groups + LATE, step_rows, wide)),
                vmem((step_rows + PAD, KINDS * width + 2 * bands)),
                vmem((everyone, 1, tile_a * tile_b)),
                vmem((everyone, 1, tile_a * tile_b)),
                dma((4,)), dma((2, groups)), dma((2, groups)), dma((2, groups)), dma((2, per_half * groups)),
                dma((2, everyone)), regular, regular,
            ],
            compiler_params=pltpu.CompilerParams(
                collective_id=0, has_side_effects=True, vmem_limit_bytes=67043328
            ),
        )(inverse_cov, channel_keep_mask, partner_ids, band_starts)
        return jnp.reshape(found, (2, tile_a, tile_b))

    placed = (P("bl", "bp", None), P("bl", None), P("bl", None), P())
    return jax.shard_map(body, mesh=mesh, in_specs=placed, out_specs=P(None, "bp", "bl"), check_vma=False)
```

time: 28.9 us -> 27.4 us (0.948)
  Pallas kernels: 27.2 us -> 25.8 us
    pallas_call x1, Pallas kernels: 27.2 us -> 25.8 us  [body(): pl.pallas_call(partial(kernel, (groups, owners, rows, width, bands, seats...]
    reshape x0 -> x2, local copies, waits for them, and re-layouts: none -> 1.44 us  [body(): return jnp.reshape(found, (2, tile_a, tile_b))]
    pallas_call x1 -> x0, local copies, waits for them, and re-layouts: 1.38 us -> none  [body(): pl.pallas_call(partial(kernel, (groups, owners, rows, width, bands, seats...]
where the time goes in v2:
time: 27.4 us; the launch traced here: 27.2 us
  Pallas kernels  25.8 us (94%)
  local copies, waits for them, and re-layouts  1.44 us (5%)
    pallas_call x1, Pallas kernels, body(): pl.pallas_call(partial(kernel, (groups, owners, rows, width, bands, seats...  25.8 us
    reshape x2, local copies, waits for them, and re-layouts, body(): return jnp.reshape(found, (2, tile_a, tile_b))  1.44 us

profile of v2, /device:TPU:0, one launch (start us, length us, event | category | flops | bytes accessed | tf_op | source)
XLA Modules:
  0.0 27.2 jit_solution(5731766939453509202)
XLA Ops:
  0.0 25.8 %fisher.1 = f32[2,128]{1,0:T(2,128)} custom-call(f32[1,256,1024]{2,1,0:T(8,128)} %cov_ref.1, s32[1,1024]{1,0:T(1,128)} %mask_ref.1, s32[1,2]{1,0:T(1,128)} %partner_ref.1, s32[2,64]{1,0:T(2,128)} %starts_ref.1), custom_call_target="tpu_custom_call" | custom-call | tf_op jit(solution)/shard_map/fisher/pallas_call | solution.py:484
  25.8 0.8 %reshape.3 = f32[2,16,8]{2,1,0:T(8,128)S(1)} reshape(f32[2,128]{1,0:T(2,128)} %fisher.1) | data formatting | bytes 2048 | tf_op jit(solution)/shard_map/reshape | solution.py:525
  26.5 0.7 %copy.6 = f32[2,16,8]{1,2,0:T(8,128)} copy(f32[2,16,8]{2,1,0:T(8,128)S(1)} %reshape.3) | data formatting | bytes 2048 | tf_op jit(solution)/shard_map/reshape | solution.py:525

commit v3 on v2

--- a/solution.py
+++ b/solution.py
@@ -128,32 +128,26 @@
         tell(barrier, (peers[d], level))
     tell_levels(barrier)
 
-    def remote(source, target, sems, n, device):
+    def remote(source, target, sems, n, device, shared=False):
         return pltpu.make_async_remote_copy(
-            src_ref=source, dst_ref=target, send_sem=sems.at[0, n], recv_sem=sems.at[1, n],
+            src_ref=source, dst_ref=target, send_sem=sems.at[0, 0 if shared else n], recv_sem=sems.at[1, n],
             device_id=device, device_id_type=MESH,
         )
 
-    sent = []
-
-    def send(copy):
-        copy.start()
-        sent.append(copy)
-
     def send_marks(d):
         n = seat_of[d]
-        send(remote(partner_row, partner_all.at[n], p_sem, n, (peers[d], level)))
-        send(remote(masks, mask_all.at[n], m_sem, n, (peers[d], level)))
+        remote(partner_row, partner_all.at[n], p_sem, 0, (peers[d], level)).start()
+        remote(masks, mask_all.at[n], m_sem, n, (peers[d], level), True).start()
 
     def send_slice(d):
         n, g = seat_of[d], peers[d]
-        send(remote(raw.at[pl.ds(pl.multiple_of(g * count, count), count)], slices.at[n], x_sem, n, (g, level)))
+        part = raw.at[pl.ds(pl.multiple_of(g * count, count), count)]
+        remote(part, slices.at[n], x_sem, n, (g, level), True).start()
 
     def send_rim(d, across):
         n, g = seat_of[d], peers[d]
         row = per_half - 1 - place if across else place
-        send(remote(
-            rim_out.at[row * groups + g], rim.at[n, :, mine], c_sem, across * groups + n, (g, levels[across])))
+        remote(rim_out.at[row * groups + g], rim.at[n, :, mine], c_sem, across, (g, levels[across])).start()
 
     def landing(target, sems, n, device):
         remote(target, target, sems, n, device).wait_recv()
@@ -298,8 +292,9 @@
     for d in others + [0]:
         send_rim(d, 1)
 
-    for n in range(1, groups):
-        landing(partner_all.at[n], p_sem, n, (peers[arrivals[n]], level))
+    partners = remote(partner_all.at[1:groups], partner_all.at[1:groups], p_sem, 0, (peers[1], level))
+    partners.wait_send()
+    partners.wait_recv()
     names = [peers[d] for d in arrivals]
     total = fixed * count
     lane_of, lane_pad = iota((1, total), 1) // count, iota((1, groups * PAD), 1) // PAD
@@ -367,14 +362,13 @@
         for k in range(KINDS):
             blended[k, t] = blended[k, t] + mutual * boxed[k, fixed + 1 - t]
 
-    for copy in sent:
-        copy.wait_send()
-    sent.clear()
-    for n in range(groups):
-        d = arrivals[n]
-        if d:
-            landing(rim.at[n, :, mine], c_sem, n, (peers[d], level))
-        landing(rim.at[n, :, other], c_sem, groups + n, (peers[d], levels[1]))
+    for target, sems in ((slices, x_sem), (mask_all, m_sem)):
+        remote(target.at[1:groups], target.at[1:groups], sems, 0, (peers[1], level)).wait_send()
+    for across, columns in ((0, mine), (1, other)):
+        ends = rim.at[1 - across:groups, :, columns]
+        rims = remote(rim_out.at[1 - across:groups], ends, c_sem, across, (peers[1], levels[across]))
+        rims.wait_send()
+        rims.wait_recv()
     blank = jnp.zeros((KINDS, width), F32)
     tops, tails = [], []
     for n in range(groups):
@@ -444,18 +438,16 @@
             tiles[z * groups + g] = packed[:, z * span:(z + 1) * span]
 
     landed[0] = tiles[level * groups + me]
-    finals = []
+    everyone = groups * owners
     for dz in reversed(range(owners)):
         for d in others + [0]:
             if dz or d:
                 n = dz * groups + d
-                copy = remote(tiles.at[levels[dz] * groups + peers[d]], landed.at[n], fin_sem, n, (peers[d], levels[dz]))
-                send(copy)
-                finals.append(copy)
-    for copy in sent:
-        copy.wait_send()
-    for copy in finals:
-        copy.wait_recv()
+                remote(
+                    tiles.at[levels[dz] * groups + peers[d]], landed.at[n], fin_sem, 0, (peers[d], levels[dz])).start()
+    finals = remote(tiles.at[1:everyone], landed.at[1:everyone], fin_sem, 0, (peers[1], level))
+    finals.wait_send()
+    finals.wait_recv()
     for side in range(2):
         part = landed[side * per_half * groups:(side + 1) * per_half * groups]
         out_ref[pl.ds(half + side - 2 * side * half, 1), :] = jnp.sum(part, axis=0)
@@ -515,8 +507,8 @@
                 vmem((step_rows + PAD, KINDS * width + 2 * bands)),
                 vmem((everyone, 1, tile_a * tile_b)),
                 vmem((everyone, 1, tile_a * tile_b)),
-                dma((4,)), dma((2, groups)), dma((2, groups)), dma((2, groups)), dma((2, per_half * groups)),
-                dma((2, everyone)), regular, regular,
+                dma((4,)), dma((2, groups)), dma((2, groups)), dma((2, 1)), dma((2, per_half)),
+                dma((2, 1)), regular, regular,
             ],
             compiler_params=pltpu.CompilerParams(
                 collective_id=0, has_side_effects=True, vmem_limit_bytes=67043328

time: 27.4 us -> 26.3 us (0.960)
  Pallas kernels: 25.8 us -> 24.7 us
    pallas_call x1, Pallas kernels: 25.8 us -> 24.7 us  [body(): pl.pallas_call(partial(kernel, (groups, owners, rows, width, bands, seats...]
where the time goes in v3:
time: 26.3 us; the launch traced here: 26.2 us
  Pallas kernels  24.7 us (94%)
  local copies, waits for them, and re-layouts  1.44 us (5%)
    pallas_call x1, Pallas kernels, body(): pl.pallas_call(partial(kernel, (groups, owners, rows, width, bands, seats...  24.7 us
    reshape x2, local copies, waits for them, and re-layouts, body(): return jnp.reshape(found, (2, tile_a, tile_b))  1.44 us

profile of v3, /device:TPU:0, one launch (start us, length us, event | category | flops | bytes accessed | tf_op | source)
XLA Modules:
  0.0 26.2 jit_solution(1739550079938934578)
XLA Ops:
  0.0 24.7 %fisher.1 = f32[2,128]{1,0:T(2,128)} custom-call(f32[1,256,1024]{2,1,0:T(8,128)} %cov_ref.1, s32[1,1024]{1,0:T(1,128)} %mask_ref.1, s32[1,2]{1,0:T(1,128)} %partner_ref.1, s32[2,64]{1,0:T(2,128)} %starts_ref.1), custom_call_target="tpu_custom_call" | custom-call | tf_op jit(solution)/shard_map/fisher/pallas_call | solution.py:476
  24.7 0.8 %reshape.3 = f32[2,16,8]{2,1,0:T(8,128)S(1)} reshape(f32[2,128]{1,0:T(2,128)} %fisher.1) | data formatting | bytes 2048 | tf_op jit(solution)/shard_map/reshape | solution.py:517
  25.5 0.7 %copy.6 = f32[2,16,8]{1,2,0:T(8,128)} copy(f32[2,16,8]{2,1,0:T(8,128)S(1)} %reshape.3) | data formatting | bytes 2048 | tf_op jit(solution)/shard_map/reshape | solution.py:517

commit v4 on v3

--- a/solution.py
+++ b/solution.py
@@ -29,6 +29,12 @@
 
 def dot3(left, right, dims):
     return dot(left[0], right[0], dims) + (dot(left[0], right[1], dims) + dot(left[1], right[0], dims))
+
+
+def stacked3(left, right):
+    rows = left[0].shape[0]
+    pairs = dot(jnp.concatenate(left, axis=0), right[0], NN)
+    return pairs[0:rows] + pairs[rows:] + dot(left[0], right[1], NN)
 
 
 def exact(left, right, dims):
@@ -226,7 +232,7 @@
 
     def filtered(value):
         n = value.shape[0]
-        found = dot3(split(value), (table[...], table_low[...]), NN)
+        found = stacked3(split(value), (table[...], table_low[...]))
         stacked = split(jnp.concatenate([value[:, 0:rows], value[:, rows:]], axis=0))
         both = jnp.concatenate(stacked, axis=0)
         results = []
@@ -343,7 +349,7 @@
 
     held_split = split(jnp.reshape(held[0:fixed], (total, wide)))
     for n in range(groups):
-        grown[n] = dot3((spread[n], spread_low[n]), held_split, NN)
+        grown[n] = stacked3((spread[n], spread_low[n]), held_split)
 
     members = list(range(fixed, groups))
     for t in range(LATE):
@@ -356,7 +362,7 @@
     absorb(members)
     for t in range(LATE):
         n = fixed + t
-        grown[groups + t] = dot3(reach_one, split(held[n]), NN)
+        grown[groups + t] = stacked3(reach_one, split(held[n]))
         mutual = weight(n, fixed + 1 - t)
         leak[groups + t] = leak[groups + t] + mutual * leak[fixed + 1 - t]
         for k in range(KINDS):

time: 26.3 us -> 26 us (0.989)
  Pallas kernels: 24.7 us -> 24.4 us
    pallas_call x1, Pallas kernels: 24.7 us -> 24.4 us  [body(): pl.pallas_call(partial(kernel, (groups, owners, rows, width, bands, seats...]
where the time goes in v4:
time: 26 us; the launch traced here: 25.9 us
  Pallas kernels  24.4 us (94%)
  local copies, waits for them, and re-layouts  1.44 us (6%)
    pallas_call x1, Pallas kernels, body(): pl.pallas_call(partial(kernel, (groups, owners, rows, width, bands, seats...  24.4 us
    reshape x2, local copies, waits for them, and re-layouts, body(): return jnp.reshape(found, (2, tile_a, tile_b))  1.44 us

profile of v4, /device:TPU:0, one launch (start us, length us, event | category | flops | bytes accessed | tf_op | source)
XLA Modules:
  0.0 25.9 jit_solution(13380524133476953327)
XLA Ops:
  0.0 24.4 %fisher.1 = f32[2,128]{1,0:T(2,128)} custom-call(f32[1,256,1024]{2,1,0:T(8,128)} %cov_ref.1, s32[1,1024]{1,0:T(1,128)} %mask_ref.1, s32[1,2]{1,0:T(1,128)} %partner_ref.1, s32[2,64]{1,0:T(2,128)} %starts_ref.1), custom_call_target="tpu_custom_call" | custom-call | tf_op jit(solution)/shard_map/fisher/pallas_call | solution.py:482
  24.4 0.8 %reshape.3 = f32[2,16,8]{2,1,0:T(8,128)S(1)} reshape(f32[2,128]{1,0:T(2,128)} %fisher.1) | data formatting | bytes 2048 | tf_op jit(solution)/shard_map/reshape | solution.py:523
  25.2 0.7 %copy.6 = f32[2,16,8]{1,2,0:T(8,128)} copy(f32[2,16,8]{2,1,0:T(8,128)S(1)} %reshape.3) | data formatting | bytes 2048 | tf_op jit(solution)/shard_map/reshape | solution.py:523
